TPU v7x, 32 devices: a whole 2x2x4 slice. The times are simulated.
32 devices in a mesh: group: 4 (over y, core), peer: 8 (over z, x).
Axes of the slice: x: 2, y: 2, z: 4, core: 2. Of those that a mesh axis runs over, the one named last changes fastest.
Arguments:
- states: float32 [41, 1048576], P(None, ('group', 'peer')), may hold values from -6 to 6
- block_part: int32 [8192], P(('group', 'peer')), may hold values from 0 to 31, as said below
- tile_perm: int32 [8192, 128], P(('group', 'peer')), may hold values from 0 to 127, each once within a row
- half_volt: float32 [40], replicated, may hold values from -4 to 4
- steepness: float32 [40], replicated, may hold values from 0.5 to 4
- gate_rate: float32 [40], replicated, may hold values from 0.1 to 1
- conductance: float32 [40], replicated, may hold values from 0.005 to 0.08
- reversal: float32 [40], replicated, may hold values from -6 to 6
Outputs:
- regrouped: float32 [41, 1048576], P(None, ('group', 'peer'))
Inputs may be any that keep to these rules, and one draw needn't show every extreme that they name: `block_part`: every partition holds exactly 256 blocks. Within each slab of 256 consecutive global blocks no partition holds more than 16 blocks; every slab has exactly 16 blocks of some partition, and every partition has exactly 16 blocks in some slab.
All inputs are finite; a program needn't handle non-finite values.
Results may differ from a plain program's by a relative error of at most 0.0001.
Values sent between devices are 32-bit elements; how exact they have to be, the bound alone decides.
No kernel may reach another device: no remote copies, remote signals or barrier semaphores. Data moves between devices by JAX's collectives and lax.ppermute only.
A program may use at most 192 MiB of HBM per device.

v0:
```python
import jax
import jax.numpy as jnp
from jax import lax
from jax.sharding import PartitionSpec as P

time_step = 0.25


def entering(part, axis, combine, identity):
    place = lax.axis_index(axis)
    gathered = lax.all_gather(part, axis)
    state = jnp.zeros_like(part) + jnp.asarray(identity, part.dtype)

    def one(step, state):
        return combine(state, lax.dynamic_index_in_dim(gathered, step, 0, False))

    return lax.fori_loop(0, place, one, state)


def advance(state_rows, half_volt, steepness, gate_rate, conductance, reversal):
    voltage = state_rows[0:1]
    gate_vals = state_rows[1:]
    steady = jax.nn.sigmoid((voltage - half_volt[:, None]) * steepness[:, None])
    damping = jnp.exp(-gate_rate[:, None] * (1.0 + jax.nn.sigmoid(voltage)))
    gate_vals = steady + (gate_vals - steady) * damping
    current = jnp.sum(
        conductance[:, None] * gate_vals * (voltage - reversal[:, None]), axis=0, keepdims=True
    )
    voltage = voltage - time_step * current
    return jnp.concatenate([voltage, gate_vals], axis=0)


def add_counts(earlier, later):
    return earlier + later


def on_device(
    states, block_part, tile_perm, half_volt, steepness, gate_rate, conductance, reversal
):
    devices = lax.axis_size(("group", "peer"))
    local_blocks = block_part.shape[0]
    tile_width = tile_perm.shape[1]
    width = states.shape[0]
    capacity = 2 * local_blocks // devices
    partitions = jnp.arange(devices, dtype=jnp.int32)
    onehot = (block_part[:, None] == partitions[None, :]).astype(jnp.int32)
    counts = jnp.sum(onehot, axis=0, dtype=jnp.int32)
    earlier = entering(counts, ("group", "peer"), add_counts, jnp.zeros_like(counts))
    rank_in = jnp.sum(
        (jnp.cumsum(onehot, axis=0, dtype=jnp.int32) - onehot) * onehot, axis=1, dtype=jnp.int32
    )
    local_index = jnp.sum(onehot * earlier[None, :], axis=1, dtype=jnp.int32) + rank_in
    slot_index = block_part * capacity + rank_in
    requests = jnp.full((devices * capacity,), -1, jnp.int32).at[slot_index].set(local_index)
    requests = requests.reshape(devices, capacity)
    advanced = advance(states, half_volt, steepness, gate_rate, conductance, reversal)
    advanced = advanced.reshape(width, local_blocks, tile_width)
    wanted = lax.all_to_all(requests, ("group", "peer"), split_axis=0, concat_axis=0, tiled=True)
    picked = jnp.maximum(wanted, 0).reshape(-1)
    served = jnp.take(advanced, picked, axis=1)
    arrived = lax.all_to_all(
        served.reshape(width, wanted.shape[0], wanted.shape[1], tile_width),
        ("group", "peer"),
        split_axis=1,
        concat_axis=1,
        tiled=True,
    )
    flat_cols = (slot_index[:, None] * tile_width + tile_perm).reshape(-1)
    return jnp.take(arrived.reshape(width, devices * capacity * tile_width), flat_cols, axis=1)


def solution(mesh):
    return jax.shard_map(
        on_device,
        mesh=mesh,
        in_specs=(
            P(None, ("group", "peer")),
            P(("group", "peer")),
            P(("group", "peer"), None),
            P(),
            P(),
            P(),
            P(),
            P(),
        ),
        out_specs=P(None, ("group", "peer")),
        check_vma=False,
    )
```

profile of v0, /device:TPU:25, one launch (start us, length us, event | category | flops | bytes accessed | tf_op | source)
XLA Modules:
  0.0 510.8 jit_solution(10718963295124107990)
XLA Ops:
  0.0 0.8 convert_reduce_fusion
  1.0 38.3 %all-reduce = s32[1024]{0:T(1024)S(1)} all-reduce(s32[1024]{0:T(1024)S(1)} %dynamic-update-slice), channel_id=2, replica_groups=mesh['group'=4,'peer'=8] {'group','peer'}, use_global_device_ids=true, to_apply=%add | all-reduce | flops 1024 | bytes 8192
  39.9 0.7 fusion.2
  40.6 0.6 reduce-window.6
  41.4 0.8 select_reduce_fusion
  42.2 0.7 broadcast_multiply_fusion.1
  42.9 1.4 scatter_custom_fusion
  44.3 0.7 all_to_all.9
  45.0 7.2 %all-to-all-start = ((s32[32,1,16]{2,1,0:T(1,128)}), s32[32,1,16]{2,1,0:T(1,128)S(1)}, u32[]{:S(2)}, u32[]{:S(2)}) async-start(s32[32,1,16]{2,1,0:T(1,128)} %bitcast.4), calls=%async_computation | async-start | bytes 32768 | tf_op jit(solution)/shard_map/all_to_all | solution.py:58
  52.1 0.7 neg.11
  52.8 1.5 divide_add_fusion
  54.3 6.4 %multiply_reduce_fusion = (f32[32768]{0:T(1024)S(1)}, f32[40,32768]{1,0:T(8,128)S(1)}) fusion(f32[40]{0:T(128)} %param.17, f32[32768]{0:T(1024)S(1)} %bitcast.45, f32[40]{0:T(128)} %param.16, f32[32768]{0:T(1024)S(1)} %bitcast.44, f32[40]{0:T(128)S(1)} %neg.11, f32[41,32768]{1,0:T(8,128)} %param.10, f32[40]{0:T(128)} %param.14, f32[40]{0:T(128)} %param.13), kind=kLoop, calls=%fused_computation.7 | loop fusion | flops 17006592 | bytes 10879776 | tf_op jit(solution)/shard_map/reduce_sum | solution.py:26
  60.7 1.3 slice_subtract_fusion
  62.6 1.1 copy.34
  63.7 0.6 slice.21
  64.2 5.9 %copy.29 = f32[41,256,128]{2,0,1:T(8,128)} copy(f32[41,256,128]{2,1,0:T(8,128)S(1)} %slice.21) | data formatting | bytes 10747904 | tf_op jit(solution)/shard_map/reshape | solution.py:57
  70.5 8.7 %gather_fusion = f32[512,41,128]{2,1,0:T(8,128)} fusion(f32[41,256,128]{2,0,1:T(8,128)} %copy.29, s32[1024]{0:T(1024)S(1)} %pad_clamp_fusion), kind=kCustom, calls=%fused_computation | custom fusion | bytes 21497856 | tf_op jit(solution)/shard_map/jit(_take)/gather | solution.py:60
  79.2 14.1 %copy_select_fusion = f32[41,32,16,128]{3,2,0,1:T(8,128)} fusion(f32[41,32,16,128]{3,0,2,1:T(8,128)} %bitcast.41, pred[32,16]{1,0:T(8,128)(4,1)S(1)} %copy.27), kind=kLoop, calls=%fused_computation.5 | loop fusion | flops 2686976 | bytes 21496320 | tf_op jit(solution)/shard_map/jit(_take)/select_n | solution.py:60
  93.3 5.9 %all-to-all-start.1 = ((f32[41,32,16,128]{3,2,0,1:T(8,128)}), f32[41,32,16,128]{3,2,0,1:T(8,128)}, u32[]{:S(2)}, u32[]{:S(2)}) async-start(f32[41,32,16,128]{3,2,0,1:T(8,128)} %copy_select_fusion), calls=%async_computation.1 | async-start | bytes 21495808 | tf_op jit(solution)/shard_map/all_to_all | solution.py:61
  99.5 240.6 %all-to-all-done.1 = f32[41,32,16,128]{3,2,0,1:T(8,128)} async-done(((f32[41,32,16,128]{3,2,0,1:T(8,128)}), f32[41,32,16,128]{3,2,0,1:T(8,128)}, u32[]{:S(2)}, u32[]{:S(2)}) %all-to-all-start.1) | async-done | bytes 10747936 | tf_op jit(solution)/shard_map/all_to_all | solution.py:61
  340.0 20.7 %copy.31 = f32[41,32,16,128]{0,3,2,1:T(8,128)} copy(f32[41,32,16,128]{3,2,0,1:T(8,128)} %all-to-all-done.1) | data formatting | bytes 21495808 | tf_op jit(solution)/shard_map/all_to_all | solution.py:61
  360.8 118.8 %gather_fusion.1 = f32[32768,41]{1,0:T(8,128)} fusion(f32[41,65536]{0,1:T(8,128)} %bitcast.40, s32[32768]{0:T(1024)S(1)} %broadcast_clamp_fusion), kind=kCustom, calls=%fused_computation.1 | custom fusion | bytes 10878976 | tf_op jit(solution)/shard_map/jit(_take)/gather | solution.py:69
  479.6 19.1 %select_bitcast_fusion = f32[41,32768]{0,1:T(8,128)} fusion(f32[32768,41]{1,0:T(8,128)} %gather_fusion.1, pred[32768]{0:T(1024)(128)(4,1)S(1)} %get-tuple-element.39), kind=kLoop, calls=%fused_computation.4 | loop fusion | flops 1343488 | bytes 10780672 | tf_op jit(solution)/shard_map/jit(_take)/select_n | solution.py:69
  498.7 12.1 %copy.32 = f32[41,32768]{1,0:T(8,128)} copy(f32[41,32768]{0,1:T(8,128)} %select_bitcast_fusion) | data formatting | bytes 10747904 | tf_op jit(solution)/shard_map/jit(_take)/select_n | solution.py:69
  (37 shorter events, 2.4 us)
Async XLA Ops:
  45.0 25.2 %all-to-all-start = ((s32[32,1,16]{2,1,0:T(1,128)}), s32[32,1,16]{2,1,0:T(1,128)S(1)}, u32[]{:S(2)}, u32[]{:S(2)}) async-start(s32[32,1,16]{2,1,0:T(1,128)} %bitcast.4), calls=%async_computation | async-start | bytes 32768 | tf_op jit(solution)/shard_map/all_to_all | solution.py:58
  93.3 5.9 %copy-start = (s32[256,128]{1,0:T(8,128)S(1)}, s32[256,128]{1,0:T(8,128)}, u32[]{:S(2)}) copy-start(s32[256,128]{1,0:T(8,128)} %param.12) | copy-start | bytes 393220
  93.3 246.8 %all-to-all-start.1 = ((f32[41,32,16,128]{3,2,0,1:T(8,128)}), f32[41,32,16,128]{3,2,0,1:T(8,128)}, u32[]{:S(2)}, u32[]{:S(2)}) async-start(f32[41,32,16,128]{3,2,0,1:T(8,128)} %copy_select_fusion), calls=%async_computation.1 | async-start | bytes 21495808 | tf_op jit(solution)/shard_map/all_to_all | solution.py:61
where the time goes:
time: 512 us; the launch traced here: 511 us
  waiting for transfers between devices  241 us (47%)
  local copies, waits for them, and re-layouts  171 us (33%)
  other arithmetic  47.6 us (9%)
  blocking collectives  38.3 us (7%)
  starting transfers between devices  13 us (3%)
    all_to_all x1, waiting for transfers between devices, on_device(): lax.all_to_all(served.reshape(width, wanted.shape[0], wanted.shape[1], ti...  241 us
    gather x1, local copies, waits for them, and re-layouts, on_device(): jnp.take(arrived.reshape(width, devices * capacity * tile_width), flat_co...  119 us
    unnamed x1, blocking collectives  38.3 us
    all_to_all x1, local copies, waits for them, and re-layouts, on_device(): lax.all_to_all(served.reshape(width, wanted.shape[0], wanted.shape[1], ti...  20.7 us
    select_n x2, other arithmetic, on_device(): jnp.take(arrived.reshape(width, devices * capacity * tile_width), flat_co...  19.2 us
    select_n x1, other arithmetic, on_device(): served = jnp.take(advanced, picked, axis=1)  14.1 us
    select_n x1, local copies, waits for them, and re-layouts, on_device(): jnp.take(arrived.reshape(width, devices * capacity * tile_width), flat_co...  12.1 us
  transfers between devices with their start and end apart: 2, of which 1 were waited for; matrix products, arithmetic and copies ran while one was open for 4% of the time, Pallas kernels for 0%

commit v1 on v0

v1 whole, which is shorter than its diff:
```python
import functools

import jax
import jax.numpy as jnp
from jax import lax
from jax.experimental import pallas as pl
from jax.experimental.pallas import tpu as pltpu
from jax.sharding import PartitionSpec as P

time_step = 0.25
sublanes = 8
both = ("group", "peer")


def advance_kernel(params_ref, states_ref, out_ref, *, step):
    rows = states_ref.shape[0]
    half_volt = params_ref[:, 0:1]
    steepness = params_ref[:, 1:2]
    gate_rate = params_ref[:, 2:3]
    conductance = params_ref[:, 3:4]
    reversal = params_ref[:, 4:5]
    row = lax.broadcasted_iota(jnp.int32, (rows, step), 0)

    def one(i, carry):
        cols = pl.ds(pl.multiple_of(i * step, step), step)
        vals = states_ref[:, cols]
        voltage = vals[0:1]
        steady = jax.nn.sigmoid((voltage - half_volt) * steepness)
        damping = jnp.exp(-gate_rate * (1.0 + jax.nn.sigmoid(voltage)))
        gates = steady + (vals - steady) * damping
        current = jnp.sum(
            conductance * gates * (voltage - reversal), axis=0, keepdims=True
        )
        out_ref[:, cols] = jnp.where(row == 0, voltage - time_step * current, gates)
        return carry

    lax.fori_loop(0, states_ref.shape[1] // step, one, 0)


def advance(states, half_volt, steepness, gate_rate, conductance, reversal):
    rows, nodes = states.shape
    params = jnp.pad(
        jnp.stack([half_volt, steepness, gate_rate, conductance, reversal], axis=1),
        ((1, 0), (0, 0)),
    )
    block = math_block(nodes, 2048)
    step = math_block(block, 256)
    return pl.pallas_call(
        functools.partial(advance_kernel, step=step),
        grid=(nodes // block,),
        in_specs=[
            pl.BlockSpec(params.shape, lambda i: (0, 0)),
            pl.BlockSpec((rows, block), lambda i: (0, i)),
        ],
        out_specs=pl.BlockSpec((rows, block), lambda i: (0, i)),
        out_shape=jax.ShapeDtypeStruct(states.shape, states.dtype),
        cost_estimate=pl.CostEstimate(
            flops=40 * rows * nodes,
            bytes_accessed=8 * rows * nodes,
            transcendentals=3 * rows * nodes,
        ),
        name="advance",
    )(params, states)


def math_block(total, most):
    size = min(total, most)
    while total % size:
        size -= 128
    return size


def pack_kernel(counts_ref, adv_ref, out_ref, start_ref, *, slots, blocks, width):
    full = adv_ref.shape[0] // sublanes * sublanes
    extra = adv_ref.shape[0] - full
    per_step = out_ref.shape[0]
    first = pl.program_id(0) * per_step

    @pl.when(first == 0)
    def _():
        start_ref[0] = 0

    start = start_ref[0]
    for d in range(per_step):
        for k in range(slots):
            block = jnp.minimum(start + k, blocks - 1)
            cols = pl.ds(pl.multiple_of(block * width, width), width)
            out_ref[d, k * full : (k + 1) * full, :] = adv_ref[0:full, cols]
            for e in range(extra):
                row = slots * full + e * slots + k
                out_ref[d, row : row + 1, :] = adv_ref[full + e : full + e + 1, cols]
        start = start + counts_ref[first + d]
    start_ref[0] = start


def pack(counts, adv, devices, slots, width):
    rows, nodes = adv.shape
    per_step = 4
    return pl.pallas_call(
        functools.partial(pack_kernel, slots=slots, blocks=nodes // width, width=width),
        grid_spec=pltpu.PrefetchScalarGridSpec(
            num_scalar_prefetch=1,
            grid=(devices // per_step,),
            in_specs=[pl.BlockSpec(adv.shape, lambda i, c: (0, 0))],
            out_specs=pl.BlockSpec((per_step, rows * slots, width), lambda i, c: (i, 0, 0)),
            scratch_shapes=[pltpu.SMEM((1,), jnp.int32)],
        ),
        out_shape=jax.ShapeDtypeStruct((devices, rows * slots, width), adv.dtype),
        name="pack",
    )(counts, adv)


def permuted(vals, lanes):
    return jnp.take_along_axis(vals, lanes, axis=1, mode="promise_in_bounds")


def unpack_kernel(part_ref, rank_ref, perm_ref, got_ref, out_ref, tail_ref, *, slots):
    rows, nodes = out_ref.shape
    per_step, width = perm_ref.shape
    full = rows // sublanes * sublanes
    first = pl.program_id(0) * per_step
    for i in range(per_step):
        part = part_ref[first + i]
        rank = rank_ref[first + i]
        lanes = jnp.broadcast_to(perm_ref[i : i + 1, :], (full, width))
        vals = got_ref[part, pl.ds(pl.multiple_of(rank * full, full), full), :]
        out_ref[0:full, i * width : (i + 1) * width] = permuted(vals, lanes)
        for e in range(rows - full):
            row = slots * full + e * slots + rank
            tail_ref[e, i : i + 1, :] = got_ref[part, pl.ds(row, 1), :]
    for e in range(rows - full):
        tail = permuted(tail_ref[e], perm_ref[...])
        for i in range(per_step):
            cols = slice(i * width, (i + 1) * width)
            out_ref[full + e : full + e + 1, cols] = tail[i : i + 1, :]


def unpack(part, rank, perm, got, rows, slots):
    blocks, width = perm.shape
    per_step = 16
    return pl.pallas_call(
        functools.partial(unpack_kernel, slots=slots),
        grid_spec=pltpu.PrefetchScalarGridSpec(
            num_scalar_prefetch=2,
            grid=(blocks // per_step,),
            in_specs=[
                pl.BlockSpec((per_step, width), lambda i, p, r: (i, 0)),
                pl.BlockSpec(got.shape, lambda i, p, r: (0, 0, 0)),
            ],
            out_specs=pl.BlockSpec((rows, per_step * width), lambda i, p, r: (0, i)),
            scratch_shapes=[
                pltpu.VMEM((max(rows % sublanes, 1), per_step, width), got.dtype)
            ],
        ),
        out_shape=jax.ShapeDtypeStruct((rows, blocks * width), got.dtype),
        name="unpack",
    )(part, rank, perm, got)


def on_device(
    states, block_part, tile_perm, half_volt, steepness, gate_rate, conductance, reversal
):
    devices = lax.axis_size(both)
    blocks, width = tile_perm.shape
    rows = states.shape[0]
    slots = 2 * blocks // devices
    partitions = jnp.arange(devices, dtype=jnp.int32)
    onehot = (block_part[:, None] == partitions[None, :]).astype(jnp.int32)
    counts = jnp.sum(onehot, axis=0, dtype=jnp.int32)
    asked = lax.all_to_all(counts, both, split_axis=0, concat_axis=0, tiled=True)
    adv = advance(states, half_volt, steepness, gate_rate, conductance, reversal)
    send = pack(asked, adv, devices, slots, width)
    got = lax.all_to_all(send, both, split_axis=0, concat_axis=0, tiled=True)
    same = block_part[:, None] == block_part[None, :]
    position = jnp.arange(blocks, dtype=jnp.int32)
    ahead = position[None, :] < position[:, None]
    rank = jnp.sum((same & ahead).astype(jnp.int32), axis=1, dtype=jnp.int32)
    return unpack(block_part, rank, tile_perm, got, rows, slots)


def solution(mesh):
    return jax.shard_map(
        on_device,
        mesh=mesh,
        in_specs=(
            P(None, both),
            P(both),
            P(both, None),
            P(),
            P(),
            P(),
            P(),
            P(),
        ),
        out_specs=P(None, both),
        check_vma=False,
    )
```

time: 512 us -> 300 us (0.59)
  local copies, waits for them, and re-layouts: 171 us -> 2.13 us
  other arithmetic: 47.6 us -> 2.76 us
  Pallas kernels: 0 us -> 41.9 us
  blocking collectives: 38.3 us -> 0 us
    gather x2 -> x0, local copies, waits for them, and re-layouts: 128 us -> none  [the longest x1 119 us: on_device(): jnp.take(arrived.reshape(width, devices * capacity * tile_width), flat_co...]
    pallas_call x0 -> x3, Pallas kernels: none -> 41.9 us  [the longest x1 18.7 us: advance(): pl.pallas_call(functools.partial(advance_kernel, step=step), grid=(nodes...]
    unnamed x1 -> x0, blocking collectives: 38.3 us -> none
    select_n x3 -> x0, other arithmetic: 33.3 us -> none  [the longest x2 19.2 us: on_device(): jnp.take(arrived.reshape(width, devices * capacity * tile_width), flat_co...]
    all_to_all x3 -> x1, local copies, waits for them, and re-layouts: 21.5 us -> 0.69 us  [on_device(): lax.all_to_all(counts, both, split_axis=0, concat_axis=0, tiled=True)]
    select_n x1 -> x0, local copies, waits for them, and re-layouts: 12.1 us -> none  [on_device(): jnp.take(arrived.reshape(width, devices * capacity * tile_width), flat_co...]
    reshape x2 -> x0, local copies, waits for them, and re-layouts: 6.46 us -> none  [on_device(): advanced = advanced.reshape(width, local_blocks, tile_width)]
    reduce_sum x2 -> x1, other arithmetic: 7.15 us -> 0.76 us  [on_device(): rank = jnp.sum((same & ahead).astype(jnp.int32), axis=1, dtype=jnp.int32)]
  transfers between devices with their start and end apart: 2 -> 2, of which waited for: 1 -> 1; matrix products, arithmetic and copies ran while one was open for 4% -> 1% of each run, Pallas kernels for 0% -> 6%
where the time goes in v1:
time: 300 us; the launch traced here: 299 us
  waiting for transfers between devices  240 us (80%)
  Pallas kernels  41.9 us (14%)
  starting transfers between devices  12 us (4%)
    all_to_all x1, waiting for transfers between devices, on_device(): got = lax.all_to_all(send, both, split_axis=0, concat_axis=0, tiled=True)  240 us
    pallas_call x1, Pallas kernels, advance(): pl.pallas_call(functools.partial(advance_kernel, step=step), grid=(nodes...  18.7 us
    pallas_call x1, Pallas kernels, unpack(): pl.pallas_call(functools.partial(unpack_kernel, slots=slots), grid_spec=p...  14 us
    pallas_call x1, Pallas kernels, pack(): pl.pallas_call(functools.partial(pack_kernel, slots=slots, blocks=nodes /...  9.11 us
    all_to_all x1, starting transfers between devices, on_device(): lax.all_to_all(counts, both, split_axis=0, concat_axis=0, tiled=True)  6.16 us
  transfers between devices with their start and end apart: 2, of which 1 were waited for; matrix products, arithmetic and copies ran while one was open for 1% of the time, Pallas kernels for 6%

profile of v1, /device:TPU:25, one launch (start us, length us, event | category | flops | bytes accessed | tf_op | source)
XLA Modules:
  0.0 298.9 jit_solution(497765008143071870)
XLA Ops:
  0.0 0.8 convert_reduce_fusion.1
  0.8 0.7 copy.18
  1.5 6.2 %all-to-all-start = ((s32[32,1,1]{2,1,0:T(1,128)}), s32[32,1,1]{2,1,0:T(1,128)S(1)}, u32[]{:S(2)}, u32[]{:S(2)}) async-start(s32[32,1,1]{2,1,0:T(1,128)} %copy.18), calls=%async_computation | async-start | bytes 32768 | tf_op jit(solution)/shard_map/all_to_all | solution.py:170
  7.7 0.7 stack.23
  8.4 0.1 copy.19
  8.5 0.6 pad.4.params_ref
  9.1 18.7 %advance.1.adv_ref = f32[41,32768]{1,0:T(8,128)} custom-call(f32[41,5]{1,0:T(8,128)} %pad.4.params_ref, f32[41,32768]{1,0:T(8,128)} %states_ref.1), custom_call_target="tpu_custom_call" | custom-call | flops 53739520 | bytes 10747904 | tf_op jit(solution)/shard_map/advance/pallas_call | solution.py:48
  27.8 0.0 all-to-all-done
  27.8 1.2 reduce.counts_ref
  29.0 9.1 %pack.1 = f32[32,656,128]{2,1,0:T(8,128)} custom-call(s32[32]{0:T(128)} %reduce.counts_ref, f32[41,32768]{1,0:T(8,128)} %advance.1.adv_ref), custom_call_target="tpu_custom_call" | custom-call | tf_op jit(solution)/shard_map/pack/pallas_call | solution.py:99
  38.2 0.0 copy-start
  38.2 5.9 %all-to-all-start.1 = ((f32[32,656,128]{2,1,0:T(8,128)}), f32[32,656,128]{2,1,0:T(8,128)}, u32[]{:S(2)}, u32[]{:S(2)}) async-start(f32[32,656,128]{2,1,0:T(8,128)} %pack.1), calls=%async_computation.1 | async-start | bytes 21495808 | tf_op jit(solution)/shard_map/all_to_all | solution.py:173
  44.0 0.0 copy-done
  44.1 0.8 convert_reduce_fusion.rank_ref
  44.8 240.1 %all-to-all-done.1.got_ref = f32[32,656,128]{2,1,0:T(8,128)} async-done(((f32[32,656,128]{2,1,0:T(8,128)}), f32[32,656,128]{2,1,0:T(8,128)}, u32[]{:S(2)}, u32[]{:S(2)}) %all-to-all-start.1) | async-done | bytes 10747936 | tf_op jit(solution)/shard_map/all_to_all | solution.py:173
  284.9 14.0 %unpack.1 = f32[41,32768]{1,0:T(8,128)} custom-call(s32[256]{0:T(256)} %part_ref.1, s32[256]{0:T(256)} %convert_reduce_fusion.rank_ref, s32[256,128]{1,0:T(8,128)} %perm_ref.1, f32[32,656,128]{2,1,0:T(8,128)} %all-to-all-done.1.got_ref), custom_call_target="tpu_custom_call" | custom-call | tf_op jit(solution)/shard_map/unpack/pallas_call | solution.py:141
Async XLA Ops:
  1.5 26.3 %all-to-all-start = ((s32[32,1,1]{2,1,0:T(1,128)}), s32[32,1,1]{2,1,0:T(1,128)S(1)}, u32[]{:S(2)}, u32[]{:S(2)}) async-start(s32[32,1,1]{2,1,0:T(1,128)} %copy.18), calls=%async_computation | async-start | bytes 32768 | tf_op jit(solution)/shard_map/all_to_all | solution.py:170
  38.2 5.9 %copy-start = (s32[256]{0:T(256)S(1)}, s32[256]{0:T(256)}, u32[]{:S(2)}) copy-start(s32[256]{0:T(256)} %part_ref.1) | copy-start | bytes 3076
  38.2 246.8 %all-to-all-start.1 = ((f32[32,656,128]{2,1,0:T(8,128)}), f32[32,656,128]{2,1,0:T(8,128)}, u32[]{:S(2)}, u32[]{:S(2)}) async-start(f32[32,656,128]{2,1,0:T(8,128)} %pack.1), calls=%async_computation.1 | async-start | bytes 21495808 | tf_op jit(solution)/shard_map/all_to_all | solution.py:173
